TPU v7x, 32 devices: a whole 2x2x4 slice. The times are simulated.
32 devices in a mesh: col: 8 (over z, y), grp: 4 (over x, core).
Axes of the slice: x: 2, y: 2, z: 4, core: 2. Of those that a mesh axis runs over, the one named last changes fastest.
Arguments:
- density_now: float32 [2, 8192, 768], P(None, ('col', 'grp')), may hold values from -6 to 6
- density_before: float32 [2, 8192, 768], P(None, ('col', 'grp')), may hold values from -6 to 6
- source: float32 [2, 8192, 768], P(None, ('col', 'grp')), may hold values from -8 to 8
- response: float32 [8192, 768], P(('col', 'grp')), may hold values from 0.5 to 4
- history_density: bfloat16 [7, 2, 8192, 768], P(None, None, ('col', 'grp')), may hold values from -6 to 6
- history_residual: bfloat16 [7, 2, 8192, 768], P(None, None, ('col', 'grp')), may hold values from -6 to 6
- column_shell: int32 [8192], P(('col', 'grp')), may hold values from 1 to 139264, as said below
- screening: float32 [1], replicated, may hold values from 1466 to 36672
Outputs:
- slab_density: float32 [2, 2, 768, 8192], P(None, None, 'col', 'grp')
- mixed_density: float32 [2, 8192, 768], P(None, ('col', 'grp'))
- residual_norm: float32 [2], replicated
Inputs may be any that keep to these rules, and one draw needn't show every extreme that they name: `column_shell`: column j's value lies between 1 + j * s and (j + 1) * s, where s = (383^2 - 1) // 8192.
All inputs are finite; a program needn't handle non-finite values.
Results may differ from a plain program's by a relative error of at most 0.0038.
Values sent between devices are 32-bit elements; how exact they have to be, the bound alone decides.
A program may use at most 192 MiB of HBM per device.

v0:
```python
import functools
import math

import jax
import jax.numpy as jnp
import numpy as np
from jax import lax
from jax.experimental import pallas as pl
from jax.experimental.pallas import tpu as pltpu
from jax.sharding import PartitionSpec as P

HIST = 8
ITERS = 2
MIXING = 0.7
ROWS = 16
CHUNK = 32
EARLY = 3
MESH = pl.DeviceIdType.MESH


def plane_table(plane_count, parts):
    slot = np.arange(plane_count)
    angle = (slot[:, None] * slot[None, :] % plane_count) * (2.0 * np.pi / plane_count)
    table = np.stack([np.cos(angle), np.sin(angle)])
    table = table.reshape(2, parts, plane_count // parts, plane_count).transpose(1, 0, 2, 3)
    table = table.reshape(parts, 2 * plane_count // parts, plane_count)
    return jnp.asarray(table.astype(np.float32)).astype(jnp.bfloat16)


def dot_rows(first, second):
    return lax.dot_general(
        first, second, (((1,), (1,)), ((), ())), preferred_element_type=jnp.float32
    )


def mix_kernel(
    n_col,
    n_grp,
    now_hbm,
    before_hbm,
    source_hbm,
    response_hbm,
    hist_rho_hbm,
    hist_res_hbm,
    shell_ref,
    screen_ref,
    table_hbm,
    slab_hbm,
    mixed_hbm,
    norm_ref,
    dens,
    source,
    response,
    rho,
    res,
    table,
    metric,
    precond,
    high,
    low,
    coef,
    gram,
    square,
    sums,
    outgoing,
    load_sem,
    late_sem,
    sums_send,
    sums_recv,
    slab_send,
    slab_recv,
    own_sem,
):
    columns, planes = response.shape
    slab = planes // n_col
    devices = n_col * n_grp
    col = lax.axis_index("col")
    grp = lax.axis_index("grp")
    me = col * n_grp + grp
    chunks = columns // CHUNK

    def peer_at(offset):
        peer = (me + offset) % devices
        return (peer // n_grp, peer % n_grp)

    barrier = pltpu.get_barrier_semaphore()

    def greet(offset, carry):
        pl.semaphore_signal(barrier, inc=1, device_id=peer_at(offset), device_id_type=MESH)
        return carry

    lax.fori_loop(1, devices, greet, 0)

    def load_copies(chunk):
        rows = pl.ds(pl.multiple_of(chunk * CHUNK, CHUNK), CHUNK)
        pairs = (
            (hist_res_hbm.at[:, :, rows, :], res.at[pl.ds(0, HIST - 1), :, rows, :]),
            (now_hbm.at[:, rows, :], dens.at[1, :, rows, :]),
            (before_hbm.at[:, rows, :], dens.at[0, :, rows, :]),
            (source_hbm.at[:, rows, :], source.at[:, rows, :]),
            (response_hbm.at[rows, :], response.at[rows, :]),
        )
        return [
            pltpu.make_async_copy(src, dst, load_sem.at[chunk, slot])
            for slot, (src, dst) in enumerate(pairs)
        ]

    def start_loads(chunk, carry):
        for copy in load_copies(chunk):
            copy.start()
        return carry

    lax.fori_loop(0, chunks, start_loads, 0)
    late_copies = (
        pltpu.make_async_copy(hist_rho_hbm, rho.at[pl.ds(0, HIST - 1)], late_sem.at[0]),
        pltpu.make_async_copy(table_hbm, table, late_sem.at[1]),
    )
    for copy in late_copies:
        copy.start()

    screen = screen_ref[0]

    def geometry(block, total):
        rows = pl.ds(pl.multiple_of(block * ROWS, ROWS), ROWS)
        slot = lax.broadcasted_iota(jnp.int32, (ROWS, planes), 1)
        signed = jnp.where(slot < planes // 2, slot, slot - planes)
        squared = shell_ref[rows, :] + signed * signed
        limit = (planes // 2 - 1) * (planes // 2 - 1)
        shells = squared.astype(jnp.float32)
        shifted = shells + screen
        value = jnp.where(squared <= limit, shifted / shells, jnp.float32(0.0))
        metric[rows, :] = value
        precond[rows, :] = MIXING * shells / shifted
        return total + value

    weights = lax.fori_loop(
        0, columns // ROWS, geometry, jnp.zeros((ROWS, planes), jnp.float32)
    )

    def whole_sum(values):
        return jnp.sum(jnp.sum(values, axis=0, keepdims=True), axis=1, keepdims=True)

    weight_local = whole_sum(weights)

    lane = lax.broadcasted_iota(jnp.int32, (HIST, 128), 1)
    row = lax.broadcasted_iota(jnp.int32, (HIST, 128), 0)

    def column_of(values, index):
        return jnp.sum(jnp.where(lane == index, values, 0.0), axis=1, keepdims=True)

    def statistics(t):
        gram[...] = jnp.zeros_like(gram)
        square[...] = jnp.zeros_like(square)

        def chunk_step(chunk, carry):
            if t == 0:
                for copy in load_copies(chunk):
                    copy.wait()
            for block in range(CHUNK // ROWS):
                rows = pl.ds(pl.multiple_of(chunk * CHUNK + block * ROWS, ROWS), ROWS)
                weight = metric[rows, :]
                gain = response[rows, :]
                for part in range(2):
                    current = dens[t + 1, part, rows, :]
                    previous = dens[t, part, rows, :]
                    constant = source[part, rows, :]
                    residual = constant - gain * current
                    earlier = constant - gain * previous
                    rho[t + HIST - 1, part, rows, :] = (current - previous).astype(jnp.bfloat16)
                    newest = (residual - earlier).astype(jnp.bfloat16)
                    res[t + HIST - 1, part, rows, :] = newest
                    stack = jnp.concatenate(
                        [res[pl.ds(t, HIST - 1), part, rows, :], newest[None]], axis=0
                    )
                    weighted = (weight[None] * stack.astype(jnp.float32)).astype(jnp.bfloat16)
                    right = jnp.concatenate(
                        [stack, residual.astype(jnp.bfloat16)[None]], axis=0
                    )
                    gram[...] += dot_rows(
                        weighted.reshape(HIST * ROWS, planes),
                        right.reshape((HIST + 1) * ROWS, planes),
                    )
                    square[...] += weight * residual * residual
            return carry

        lax.fori_loop(0, chunks, chunk_step, 0)
        shape = gram.shape
        same = (
            lax.broadcasted_iota(jnp.int32, shape, 0) % ROWS
            == lax.broadcasted_iota(jnp.int32, shape, 1) % ROWS
        )
        folded = jnp.where(same, gram[...], 0.0).reshape(HIST, ROWS, shape[1]).sum(axis=1)
        entry = lax.broadcasted_iota(jnp.int32, folded.shape, 1) // ROWS
        partial = jnp.zeros((HIST, 128), jnp.float32)
        for index in range(HIST + 1):
            total = jnp.sum(jnp.where(entry == index, folded, 0.0), axis=1, keepdims=True)
            partial = jnp.where(lane == index, total, partial)
        partial = jnp.where(lane == HIST + 1, whole_sum(square[...]), partial)
        partial = jnp.where(lane == HIST + 2, weight_local, partial)
        sums[t, me] = partial

    def sum_copy(t, offset, slot):
        return pltpu.make_async_remote_copy(
            src_ref=sums.at[t, me],
            dst_ref=sums.at[t, slot],
            send_sem=sums_send.at[t, offset],
            recv_sem=sums_recv.at[t, offset],
            device_id=peer_at(offset),
            device_id_type=MESH,
        )

    def send_sums(t):
        def step(offset, carry):
            sum_copy(t, offset, me).start()
            return carry

        lax.fori_loop(1, devices, step, 0)

    def take_sums(t):
        def step(offset, carry):
            sum_copy(t, offset, (me - offset + devices) % devices).wait()
            return carry

        lax.fori_loop(1, devices, step, 0)

    def solve(t):
        total = jnp.sum(sums[t], axis=0)
        norm_ref[pl.ds(t, 1), :] = jnp.broadcast_to(
            jnp.sqrt(column_of(total, HIST + 1) / column_of(total, HIST + 2))[:1], (1, 128)
        )
        flipped = jnp.concatenate([total] * (128 // HIST), axis=0).T[:HIST]
        system = jnp.where(lane < HIST, 0.5 * (total + flipped), total)
        for pivot in range(HIST):
            pivot_row = jnp.sum(jnp.where(row == pivot, system, 0.0), axis=0, keepdims=True)
            root = jnp.sqrt(
                jnp.sum(jnp.where(lane[:1] == pivot, pivot_row, 0.0), axis=1, keepdims=True)
            )
            factor = column_of(system, pivot) / root
            system = jnp.where(row == pivot, system, system - factor * (pivot_row / root))
        diagonal = jnp.sum(jnp.where(lane == row, system, 0.0), axis=1, keepdims=True)
        coef[...] = jnp.broadcast_to(column_of(system, HIST) / diagonal, coef.shape)

    def update(t):
        def block_step(block, carry):
            rows = pl.ds(pl.multiple_of(block * ROWS, ROWS), ROWS)
            inside = metric[rows, :] > 0.0
            gain = response[rows, :]
            scale = precond[rows, :]
            for part in range(2):
                current = dens[t + 1, part, rows, :]
                rho_mix = current
                res_mix = source[part, rows, :] - gain * current
                for entry in range(HIST):
                    weight = coef[pl.ds(entry, 1), :]
                    rho_mix = rho_mix - weight * rho[t + entry, part, rows, :].astype(jnp.float32)
                    res_mix = res_mix - weight * res[t + entry, part, rows, :].astype(jnp.float32)
                fresh = jnp.where(inside, rho_mix + scale * res_mix, 0.0)
                dens[t + 2, part, rows, :] = fresh
                top = fresh.astype(jnp.bfloat16)
                spot = pl.ds(pl.multiple_of(part * columns + block * ROWS, ROWS), ROWS)
                high[spot, :] = top
                low[spot, :] = (fresh - top.astype(jnp.float32)).astype(jnp.bfloat16)
            return carry

        lax.fori_loop(0, columns // ROWS, block_step, 0)

    def slab_copy(t, offset, origin):
        target = (col + offset) % n_col
        return pltpu.make_async_remote_copy(
            src_ref=outgoing.at[t, offset],
            dst_ref=slab_hbm.at[t, :, :, pl.ds(pl.multiple_of(origin * columns, 128), columns)],
            send_sem=slab_send.at[t, offset],
            recv_sem=slab_recv.at[t, offset],
            device_id=(target, grp),
            device_id_type=MESH,
        )

    def own_copy(t):
        return pltpu.make_async_copy(
            outgoing.at[t, 0],
            slab_hbm.at[t, :, :, pl.ds(pl.multiple_of(col * columns, 128), columns)],
            own_sem.at[t],
        )

    def transform(t, offset):
        lines = table[(col + offset) % n_col]
        products = dot_rows(lines, high[...]) + dot_rows(lines, low[...])
        products = products * jnp.float32(1.0 / math.sqrt(planes))
        cosine = products[:slab]
        sine = products[slab:]
        outgoing[t, offset, 0] = cosine[:, :columns] - sine[:, columns:]
        outgoing[t, offset, 1] = sine[:, :columns] + cosine[:, columns:]

    def send_slabs(t, first, last):
        def step(index, carry):
            offset = n_col // 2 + (1 - 2 * (index % 2)) * ((index + 1) // 2)
            transform(t, offset)
            slab_copy(t, offset, col).start()
            return carry

        lax.fori_loop(first, last, step, 0)

    statistics(0)
    pl.semaphore_wait(barrier, devices - 1)
    send_sums(0)
    for copy in late_copies:
        copy.wait()
    take_sums(0)
    solve(0)
    update(0)
    send_slabs(0, 0, EARLY)
    statistics(1)
    send_sums(1)
    send_slabs(0, EARLY, n_col - 1)
    transform(0, 0)
    own_copy(0).start()
    take_sums(1)
    solve(1)
    update(1)
    mixed_copy = pltpu.make_async_copy(dens.at[ITERS + 1], mixed_hbm, own_sem.at[ITERS])
    mixed_copy.start()
    send_slabs(1, 0, n_col - 1)
    transform(1, 0)
    own_copy(1).start()

    for t in range(ITERS):

        def finish(offset, carry):
            slab_copy(t, offset, (col - offset + n_col) % n_col).wait()
            return carry

        lax.fori_loop(1, n_col, finish, 0)
        own_copy(t).wait()
    mixed_copy.wait()


def body(
    n_col,
    n_grp,
    density_now,
    density_before,
    source,
    response,
    history_density,
    history_residual,
    column_shell,
    screening,
):
    _, columns, planes = density_now.shape
    slab = planes // n_col
    devices = n_col * n_grp
    table = plane_table(planes, n_col)
    f32, bf16 = jnp.float32, jnp.bfloat16
    any_space = pl.BlockSpec(memory_space=pl.ANY)
    vmem_space = pl.BlockSpec(memory_space=pltpu.VMEM)
    slab_out, mixed, norms = pl.pallas_call(
        functools.partial(mix_kernel, n_col, n_grp),
        out_shape=(
            jax.ShapeDtypeStruct((ITERS, 2, slab, n_col * columns), f32),
            jax.ShapeDtypeStruct((2, columns, planes), f32),
            jax.ShapeDtypeStruct((8, 128), f32),
        ),
        in_specs=[any_space] * 6
        + [vmem_space, pl.BlockSpec(memory_space=pltpu.SMEM), any_space],
        out_specs=(any_space, any_space, vmem_space),
        scratch_shapes=[
            pltpu.VMEM((ITERS + 2, 2, columns, planes), f32),
            pltpu.VMEM((2, columns, planes), f32),
            pltpu.VMEM((columns, planes), f32),
            pltpu.VMEM((HIST + ITERS - 1, 2, columns, planes), bf16),
            pltpu.VMEM((HIST + ITERS - 1, 2, columns, planes), bf16),
            pltpu.VMEM(table.shape, bf16),
            pltpu.VMEM((columns, planes), f32),
            pltpu.VMEM((columns, planes), f32),
            pltpu.VMEM((2 * columns, planes), bf16),
            pltpu.VMEM((2 * columns, planes), bf16),
            pltpu.VMEM((HIST, planes), f32),
            pltpu.VMEM((HIST * ROWS, (HIST + 1) * ROWS), f32),
            pltpu.VMEM((ROWS, planes), f32),
            pltpu.VMEM((ITERS, devices, HIST, 128), f32),
            pltpu.VMEM((ITERS, n_col, 2, slab, columns), f32),
            pltpu.SemaphoreType.DMA((columns // CHUNK, 5)),
            pltpu.SemaphoreType.DMA((2,)),
            pltpu.SemaphoreType.DMA((ITERS, devices)),
            pltpu.SemaphoreType.DMA((ITERS, devices)),
            pltpu.SemaphoreType.DMA((ITERS, n_col)),
            pltpu.SemaphoreType.DMA((ITERS, n_col)),
            pltpu.SemaphoreType.DMA((ITERS + 1,)),
        ],
        compiler_params=pltpu.CompilerParams(
            collective_id=0, has_side_effects=True, vmem_limit_bytes=60 * 1024 * 1024
        ),
    )(
        density_now,
        density_before,
        source,
        response,
        history_density,
        history_residual,
        column_shell[:, None],
        screening,
        table,
    )
    return (slab_out, mixed, norms[:ITERS, 0])


def solution(mesh):
    return jax.shard_map(
        functools.partial(body, mesh.shape["col"], mesh.shape["grp"]),
        mesh=mesh,
        in_specs=(
            P(None, ("col", "grp"), None),
            P(None, ("col", "grp"), None),
            P(None, ("col", "grp"), None),
            P(("col", "grp"), None),
            P(None, None, ("col", "grp"), None),
            P(None, None, ("col", "grp"), None),
            P(("col", "grp")),
            P(),
        ),
        out_specs=(P(None, None, "col", "grp"), P(None, ("col", "grp"), None), P()),
        check_vma=False,
    )
```

profile of v0, /device:TPU:19, one launch (start us, length us, event | category | flops | bytes accessed | tf_op | source)
XLA Modules:
  0.0 105.7 jit_solution(17246895811883034640)
XLA Ops:
  1.3 1.5 %copy.12.shell_ref = s32[256,1]{1,0:T(8,128)} copy(s32[256,1]{0,1:T(1,128)} %bitcast.1) | data formatting | bytes 2048 | tf_op jit(solution)/shard_map/broadcast_in_dim | solution.py:400
  2.8 96.5 %shard_map.112 = (f32[2,2,96,2048]{3,2,1,0:T(8,128)}, f32[2,256,768]{2,1,0:T(8,128)}, f32[8,128]{1,0:T(8,128)}) custom-call(f32[2,256,768]{2,1,0:T(8,128)} %now_hbm.1, f32[2,256,768]{2,1,0:T(8,128)} %before_hbm.1, f32[2,256,768]{2,1,0:T(8,128)} %source_hbm.1, f32[256,768]{1,0:T(8,128)} %response_hbm.1, bf16[7,2,256,768]{3,2,1,0:T(8,128)(2,1)} %hist_rho_hbm.1, ...), custom_call_target="tpu_custom_call" | custom-call | tf_op jit(solution)/shard_map/pallas_call | solution.py:356
  99.2 1.3 %slice_reduce_fusion = f32[2]{0:T(128)} fusion(f32[8,128]{1,0:T(8,128)} %get-tuple-element.8), kind=kLoop, calls=%fused_computation | loop fusion | bytes 16 | tf_op jit(solution)/shard_map/slice | solution.py:404
  100.5 0.0 copy-start
  100.5 4.0 %copy.16 = f32[2,2,96,2048]{3,2,1,0:T(8,128)} copy(f32[2,2,96,2048]{3,2,1,0:T(8,128)} %get-tuple-element.12) | data formatting | bytes 6291456
  104.6 0.0 copy-done
  104.6 1.1 %copy.17 = f32[2,256,768]{2,1,0:T(8,128)} copy(f32[2,256,768]{2,1,0:T(8,128)S(1)} %copy-done) | data formatting | bytes 3145728
Async XLA Ops:
  100.5 4.0 %copy-start = (f32[2,256,768]{2,1,0:T(8,128)S(1)}, f32[2,256,768]{2,1,0:T(8,128)}, u32[]{:S(2)}) copy-start(f32[2,256,768]{2,1,0:T(8,128)} %get-tuple-element.13) | copy-start | bytes 4718596
where the time goes:
time: 106 us
  Pallas kernels  96.5 us (91%)
  local copies, waits for them, and re-layouts  7.94 us (7%)
  between operations  1.29 us (1%)
    pallas_call x1, Pallas kernels, body(): pl.pallas_call(functools.partial(mix_kernel, n_col, n_grp), out_shape=(ja...  96.5 us
    unnamed x4, local copies, waits for them, and re-layouts  5.17 us

commit v1 on v0

--- a/solution.py
+++ b/solution.py
@@ -61,6 +61,7 @@
     coef,
     gram,
     square,
+    shells_down,
     sums,
     outgoing,
     load_sem,
@@ -119,12 +120,14 @@
         copy.start()
 
     screen = screen_ref[0]
+    shell_row = shell_ref[...].astype(jnp.float32)
+    shells_down[...] = jnp.broadcast_to(shell_row, (128, columns)).T
 
     def geometry(block, total):
         rows = pl.ds(pl.multiple_of(block * ROWS, ROWS), ROWS)
         slot = lax.broadcasted_iota(jnp.int32, (ROWS, planes), 1)
         signed = jnp.where(slot < planes // 2, slot, slot - planes)
-        squared = shell_ref[rows, :] + signed * signed
+        squared = shells_down[rows, :1].astype(jnp.int32) + signed * signed
         limit = (planes // 2 - 1) * (planes // 2 - 1)
         shells = squared.astype(jnp.float32)
         shifted = shells + screen
@@ -225,9 +228,8 @@
 
     def solve(t):
         total = jnp.sum(sums[t], axis=0)
-        norm_ref[pl.ds(t, 1), :] = jnp.broadcast_to(
-            jnp.sqrt(column_of(total, HIST + 1) / column_of(total, HIST + 2))[:1], (1, 128)
-        )
+        norm = jnp.sqrt(column_of(total, HIST + 1) / column_of(total, HIST + 2))
+        norm_ref[t] = norm[0, 0]
         flipped = jnp.concatenate([total] * (128 // HIST), axis=0).T[:HIST]
         system = jnp.where(lane < HIST, 0.5 * (total + flipped), total)
         for pivot in range(HIST):
@@ -358,11 +360,11 @@
         out_shape=(
             jax.ShapeDtypeStruct((ITERS, 2, slab, n_col * columns), f32),
             jax.ShapeDtypeStruct((2, columns, planes), f32),
-            jax.ShapeDtypeStruct((8, 128), f32),
+            jax.ShapeDtypeStruct((ITERS,), f32),
         ),
         in_specs=[any_space] * 6
         + [vmem_space, pl.BlockSpec(memory_space=pltpu.SMEM), any_space],
-        out_specs=(any_space, any_space, vmem_space),
+        out_specs=(any_space, any_space, pl.BlockSpec(memory_space=pltpu.SMEM)),
         scratch_shapes=[
             pltpu.VMEM((ITERS + 2, 2, columns, planes), f32),
             pltpu.VMEM((2, columns, planes), f32),
@@ -377,6 +379,7 @@
             pltpu.VMEM((HIST, planes), f32),
             pltpu.VMEM((HIST * ROWS, (HIST + 1) * ROWS), f32),
             pltpu.VMEM((ROWS, planes), f32),
+            pltpu.VMEM((columns, 128), f32),
             pltpu.VMEM((ITERS, devices, HIST, 128), f32),
             pltpu.VMEM((ITERS, n_col, 2, slab, columns), f32),
             pltpu.SemaphoreType.DMA((columns // CHUNK, 5)),
@@ -397,11 +400,11 @@
         response,
         history_density,
         history_residual,
-        column_shell[:, None],
+        column_shell[None, :],
         screening,
         table,
     )
-    return (slab_out, mixed, norms[:ITERS, 0])
+    return (slab_out, mixed, norms)
 
 
 def solution(mesh):

time: 106 us -> 103 us (0.972)
  local copies, waits for them, and re-layouts: 7.94 us -> 5.69 us
    broadcast_in_dim x1 -> x0, local copies, waits for them, and re-layouts: 1.47 us -> none  [body(): column_shell[:, None]]
    slice x1 -> x0, local copies, waits for them, and re-layouts: 1.3 us -> none  [body(): return (slab_out, mixed, norms[:ITERS, 0])]
    unnamed x4 -> x7, local copies, waits for them, and re-layouts: 5.17 us -> 5.69 us
where the time goes in v1:
time: 103 us
  Pallas kernels  96.1 us (93%)
  local copies, waits for them, and re-layouts  5.69 us (6%)
  between operations  1.3 us (1%)
    pallas_call x1, Pallas kernels, body(): pl.pallas_call(functools.partial(mix_kernel, n_col, n_grp), out_shape=(ja...  96.1 us
    unnamed x7, local copies, waits for them, and re-layouts  5.69 us

profile of v1, /device:TPU:19, one launch (start us, length us, event | category | flops | bytes accessed | tf_op | source)
XLA Modules:
  0.0 103.1 jit_solution(4293338337048968314)
XLA Ops:
  1.3 96.1 %shard_map.112 = (f32[2,2,96,2048]{3,2,1,0:T(8,128)}, f32[2,256,768]{2,1,0:T(8,128)}, f32[2]{0:T(128)}) custom-call(f32[2,256,768]{2,1,0:T(8,128)} %now_hbm.1, f32[2,256,768]{2,1,0:T(8,128)} %before_hbm.1, f32[2,256,768]{2,1,0:T(8,128)} %source_hbm.1, f32[256,768]{1,0:T(8,128)} %response_hbm.1, bf16[7,2,256,768]{3,2,1,0:T(8,128)(2,1)} %hist_rho_hbm.1, ...), custom_call_target="tpu_custom_call" | custom-call | tf_op jit(solution)/shard_map/pallas_call | solution.py:358
  97.4 0.0 copy-start
  97.4 4.0 %copy.16 = f32[2,2,96,2048]{3,2,1,0:T(8,128)} copy(f32[2,2,96,2048]{3,2,1,0:T(8,128)} %get-tuple-element.6) | data formatting | bytes 6291456
  101.4 0.0 copy-done
  101.4 0.0 copy-start.1
  101.4 1.1 %copy.17 = f32[2,256,768]{2,1,0:T(8,128)} copy(f32[2,256,768]{2,1,0:T(8,128)S(1)} %copy-done) | data formatting | bytes 3145728
  102.6 0.0 copy-done.1
  102.6 0.5 copy.18
Async XLA Ops:
  97.4 4.0 %copy-start = (f32[2,256,768]{2,1,0:T(8,128)S(1)}, f32[2,256,768]{2,1,0:T(8,128)}, u32[]{:S(2)}) copy-start(f32[2,256,768]{2,1,0:T(8,128)} %get-tuple-element.7) | copy-start | bytes 4718596
  101.4 1.1 %copy-start.1 = (f32[2]{0:T(128)S(1)}, f32[2]{0:T(128)}, u32[]{:S(2)}) copy-start(f32[2]{0:T(128)} %get-tuple-element.8) | copy-start | bytes 28
